TPU v7x, 128 devices: a whole 4x4x4 slice. The times are simulated.
128 devices in a mesh: stage: 2 (over core), expert: 64 (over z, y, x).
Axes of the slice: x: 4, y: 4, z: 4, core: 2. Of those that a mesh axis runs over, the one named last changes fastest.
Arguments:
- x_act: bfloat16 [2, 32768, 256], P('stage', 'expert')
- route_idx: int32 [2, 32768, 2], P('stage', 'expert')
- route_gate: float32 [2, 32768, 2], P('stage', 'expert')
- w_up: bfloat16 [2, 64, 256, 2048], P('stage', 'expert')
- w_lin: bfloat16 [2, 64, 256, 2048], P('stage', 'expert')
- w_down: bfloat16 [2, 64, 2048, 256], P('stage', 'expert')
- dy_out: bfloat16 [2, 32768, 256], P('stage', 'expert')
Outputs:
- output 1: bfloat16 [2, 32768, 256], P('stage', 'expert')
- output 2: bfloat16 [2, 32768, 256], P('stage', 'expert')
- output 3: bfloat16 [2, 64, 256, 2048], P('stage', 'expert')
- output 4: bfloat16 [2, 64, 256, 2048], P('stage', 'expert')
- output 5: bfloat16 [2, 64, 2048, 256], P('stage', 'expert')
All inputs are finite; a program needn't handle non-finite values.
Results may differ from a plain program's by a relative error of at most 0.001.
Values are sent between devices in bfloat16 or wider.
A program may use at most 1 GiB of HBM per device.

v0:
```python
import functools

import jax
import jax.numpy as jnp
from jax import lax
from jax.experimental import pallas as pl
from jax.experimental.pallas import tpu as pltpu
from jax.sharding import PartitionSpec as P

MESH = pl.DeviceIdType.MESH
F32 = jnp.float32
BF16 = jnp.bfloat16
CAP = 32
GRP = 8
ROWS = GRP * CAP
FT = 256
NT = (((1,), (1,)), ((), ()))
TN = (((0,), (0,)), ((), ()))


def torus_step(pos, q, sign):
    a, b, c = lax.div(q, 16), lax.rem(lax.div(q, 4), 4), lax.rem(q, 4)
    step_x, step_y, step_z = c, lax.rem(c + a, 4), lax.rem(c + b, 4)
    if sign < 0:
        step_x, step_y, step_z = 4 - step_x, 4 - step_y, 4 - step_z
    z = lax.rem(lax.div(pos, 16) + step_z, 4)
    y = lax.rem(lax.rem(lax.div(pos, 4), 4) + step_y, 4)
    x = lax.rem(lax.rem(pos, 4) + step_x, 4)
    return z * 16 + y * 4 + x


def slot_ids(me, group, shape, dim):
    n = lax.broadcasted_iota(jnp.int32, shape, dim)
    q = n // CAP + group * GRP
    a, b, c = q >> 4, (q >> 2) & 3, q & 3
    z = (me // 16 + c + b) & 3
    y = (me // 4 + c + a) & 3
    x = (me + c) & 3
    return ((z * 16 + y * 4 + x) * CAP + (n & (CAP - 1))).astype(F32)


def moe_kernel(
    idx_hbm, gate_hbm, x_hbm, dy_hbm, wup_hbm, wlin_hbm, wdn_hbm,
    y_hbm, dx_hbm, gup_hbm, glin_hbm, gdn_hbm,
    idx_v, gate_v, x_v, dy_v, wup, wlin, wdn,
    xs, xr, us, ur, os, orr, ds, dr,
    hid, dup, dlin, own, par, col_own, col_par,
    sum0, sum1, sumx, gup, glin, gdn, y_v, dx_v,
    in_sem, out_sem, send_sem, x_sem, u_sem, o_sem, d_sem, pack_sem,
):
    me = lax.axis_index("expert")
    stage = lax.axis_index("stage")
    other = 1 - stage
    tokens = x_v.shape[0]
    experts = wup_experts = 64
    groups = experts // GRP
    ff = wup.shape[1]

    loads = [
        pltpu.make_async_copy(src, dst, in_sem.at[n])
        for n, (src, dst) in enumerate(
            ((idx_hbm, idx_v), (x_hbm, x_v), (gate_hbm, gate_v), (dy_hbm, dy_v), (wup_hbm, wup), (wlin_hbm, wlin), (wdn_hbm, wdn))
        )
    ]
    for load in loads:
        load.start()

    barrier = pltpu.get_barrier_semaphore()

    def greet(q, carry):
        peer = torus_step(me, q, 1)
        pl.semaphore_signal(barrier, inc=1, device_id=(other, peer), device_id_type=MESH)

        @pl.when(q > 0)
        def _():
            pl.semaphore_signal(barrier, inc=1, device_id=(stage, peer), device_id_type=MESH)

        return carry

    lax.fori_loop(0, experts, greet, 0)

    def copy_of(src, dst, kind, sem, group, place, dest_stage, sign):
        q = group * GRP + place
        rows = pl.ds(pl.multiple_of(q * CAP, CAP), CAP)
        return pltpu.make_async_remote_copy(
            src_ref=src.at[rows],
            dst_ref=dst.at[rows],
            send_sem=send_sem.at[kind],
            recv_sem=sem.at[group],
            device_id=(dest_stage, torus_step(me, q, sign)),
            device_id_type=MESH,
        )

    def send_group(src, dst, kind, sem, group, dest_stage, sign, skip_self):
        for place in range(GRP):
            if place == 0 and skip_self:

                @pl.when(group > 0)
                def _():
                    copy_of(src, dst, kind, sem, group, 0, dest_stage, sign).start()
            else:
                copy_of(src, dst, kind, sem, group, place, dest_stage, sign).start()

    def wait_rows(buf, sem, rows):
        pltpu.make_async_copy(buf.at[pl.ds(0, rows)], buf.at[pl.ds(0, rows)], sem).wait()

    def wait_group(buf, sem, group, skip_self):
        if not skip_self:
            wait_rows(buf, sem.at[group], ROWS)
            return

        @pl.when(group == 0)
        def _():
            wait_rows(buf, sem.at[0], ROWS - CAP)

        @pl.when(group > 0)
        def _():
            wait_rows(buf, sem.at[group], ROWS)

    send_x = functools.partial(send_group, xs, xr, 0, x_sem, dest_stage=other, sign=1, skip_self=False)
    send_u = functools.partial(send_group, us, ur, 1, u_sem, dest_stage=stage, sign=1, skip_self=True)
    send_o = functools.partial(send_group, os, orr, 2, o_sem, dest_stage=stage, sign=-1, skip_self=True)
    send_d = functools.partial(send_group, ds, dr, 3, d_sem, dest_stage=other, sign=-1, skip_self=False)

    loads[0].wait()
    expert_row = lax.broadcasted_iota(jnp.int32, (experts, tokens), 0)
    chosen = [(idx_v[pl.ds(j, 1), :] == expert_row).astype(F32) for j in range(2)]
    before = lax.broadcasted_iota(jnp.int32, (tokens, tokens), 0) < lax.broadcasted_iota(jnp.int32, (tokens, tokens), 1)
    earlier = jnp.dot(
        (chosen[0] + chosen[1]).astype(BF16), jnp.where(before, 1.0, 0.0).astype(BF16), preferred_element_type=F32
    )
    place = earlier + CAP * expert_row.astype(F32)
    loads[2].wait()
    for j in range(2):
        own[pl.ds(j, 1), :] = jnp.sum(chosen[j] * place, axis=0, keepdims=True)
        own[pl.ds(2 + j, 1), :] = gate_v[pl.ds(j, 1), :]
    own[pl.ds(4, 4), :] = jnp.zeros((4, tokens), F32)

    def slot_mask(route, group):
        slots = slot_ids(me, group, (ROWS, 128), 0)
        slots = jnp.concatenate([slots] * (tokens // 128), axis=1)
        return [slots == route[pl.ds(j, 1), :] for j in range(2)]

    def rows_of(group):
        return pl.ds(pl.multiple_of(group * ROWS, ROWS), ROWS)

    def x_block(group):
        hit = slot_mask(own, group)
        pick = jnp.where(hit[0] | hit[1], 1.0, 0.0).astype(BF16)
        xs[rows_of(group), :] = jnp.dot(pick, x_v[...], preferred_element_type=F32).astype(BF16)

    def u_block(group):
        hit = slot_mask(par, group)
        pick = jnp.where(hit[0] | hit[1], 1.0, 0.0).astype(BF16)
        gates = jnp.where(hit[0], par[pl.ds(2, 1), :], 0.0) + jnp.where(hit[1], par[pl.ds(3, 1), :], 0.0)
        gates = jnp.sum(gates, axis=1, keepdims=True)
        rows = jnp.dot(pick, dy_v[...], preferred_element_type=F32)
        us[rows_of(group), :] = (gates * rows).astype(BF16)

    loads[1].wait()
    x_block(0)
    x_block(1)
    pl.semaphore_wait(barrier, 2 * experts - 1)
    pack = pltpu.make_async_remote_copy(
        src_ref=own, dst_ref=par, send_sem=pack_sem.at[0], recv_sem=pack_sem.at[1],
        device_id=(other, me), device_id_type=MESH,
    )
    pack.start()
    send_x(0)
    x_block(2)
    send_x(1)
    loads[3].wait()
    pack.wait()

    def feed(group, carry):
        u_block(group)

        @pl.when(group + 3 < groups)
        def _():
            x_block(group + 3)

        @pl.when(group + 2 < groups)
        def _():
            send_x(group + 2)

        @pl.when(group > 0)
        def _():
            send_u(group - 1)

        @pl.when(group == 0)
        def _():
            ur[pl.ds(0, CAP), :] = us[pl.ds(0, CAP), :]

        return carry

    lax.fori_loop(0, groups, feed, 0)

    for route, cols, count in ((own, col_own, 2), (par, col_par, 4)):
        wide = jnp.concatenate([route[...], jnp.zeros((120, tokens), F32)], axis=0)
        tall = jnp.transpose(wide, (1, 0))
        for j in range(count):
            cols[j] = jnp.broadcast_to(tall[:, j : j + 1], (tokens, 128))
    send_u(groups - 1)
    for n in range(4, 7):
        loads[n].wait()

    def work(group, carry):
        rows = rows_of(group)
        wait_group(xr, x_sem, group, False)
        wait_group(ur, u_sem, group, True)
        x_in, u_in = xr[rows, :], ur[rows, :]
        for n in range(ff // FT):
            cols = pl.ds(n * FT, FT)
            pre_up = jnp.dot(x_in, wup[:, cols], preferred_element_type=F32)
            pre_lin = jnp.dot(x_in, wlin[:, cols], preferred_element_type=F32)
            d_hid = lax.dot_general(u_in, wdn[cols, :], NT, preferred_element_type=F32).astype(BF16).astype(F32)
            sig = jax.nn.sigmoid(pre_up)
            act = pre_up * sig
            hid[rows, cols] = (act * pre_lin).astype(BF16)
            dup[rows, cols] = (d_hid * pre_lin * sig * (1.0 + pre_up * (1.0 - sig))).astype(BF16)
            dlin[rows, cols] = (d_hid * act).astype(BF16)
        os[rows, :] = jnp.dot(hid[rows, :], wdn[...], preferred_element_type=F32).astype(BF16)

        @pl.when(group == 0)
        def _():
            orr[pl.ds(0, CAP), :] = os[pl.ds(0, CAP), :]

        d_in = lax.dot_general(dup[rows, :], wup[...], NT, preferred_element_type=F32)
        d_in += lax.dot_general(dlin[rows, :], wlin[...], NT, preferred_element_type=F32)
        send_o(group)
        ds[rows, :] = d_in.astype(BF16)

        @pl.when(group > 0)
        def _():
            send_d(group - 1)

        return carry

    lax.fori_loop(0, groups, work, 0)

    def weight_grads(n, carry):
        cols = pl.ds(pl.multiple_of(n * 256, 256), 256)
        gup[:, cols] = lax.dot_general(xr[...], dup[:, cols], TN, preferred_element_type=F32).astype(BF16)
        glin[:, cols] = lax.dot_general(xr[...], dlin[:, cols], TN, preferred_element_type=F32).astype(BF16)
        g_t = lax.dot_general(ur[...], hid[:, cols], TN, preferred_element_type=F32)
        gdn[cols, :] = jnp.transpose(g_t, (1, 0)).astype(BF16)

        @pl.when(n == 0)
        def _():
            send_d(groups - 1)

        return carry

    lax.fori_loop(0, ff // 256, weight_grads, 0)
    stores = [
        pltpu.make_async_copy(src, dst, out_sem.at[n])
        for n, (src, dst) in enumerate(((gup, gup_hbm), (glin, glin_hbm), (gdn, gdn_hbm), (y_v, y_hbm), (dx_v, dx_hbm)))
    ]
    for n in range(3):
        stores[n].start()

    sum0[...] = jnp.zeros_like(sum0)
    sum1[...] = jnp.zeros_like(sum1)
    sumx[...] = jnp.zeros_like(sumx)

    def merge(group, carry):
        rows = rows_of(group)
        slots = slot_ids(me, group, (8, ROWS), 1)[0:1, :]

        def token_mask(cols, j):
            return jnp.concatenate([cols[j]] * (ROWS // 128), axis=1) == slots

        wait_group(orr, o_sem, group, True)
        for j, total in enumerate((sum0, sum1)):
            pick = jnp.where(token_mask(col_par, j), 1.0, 0.0).astype(BF16)
            total[...] += jnp.dot(pick, orr[rows, :], preferred_element_type=F32)
        wait_group(dr, d_sem, group, False)
        pick = jnp.where(token_mask(col_own, 0) | token_mask(col_own, 1), 1.0, 0.0).astype(BF16)
        sumx[...] += jnp.dot(pick, dr[rows, :], preferred_element_type=F32)
        return carry

    lax.fori_loop(0, groups, merge, 0)
    g0 = jnp.concatenate([col_par[2]] * 2, axis=1)
    g1 = jnp.concatenate([col_par[3]] * 2, axis=1)
    y_v[...] = (g0 * sum0[...] + g1 * sum1[...]).astype(BF16)
    dx_v[...] = sumx[...].astype(BF16)
    stores[3].start()
    stores[4].start()
    wait_rows(xs, send_sem.at[0], experts * CAP)
    wait_rows(us, send_sem.at[1], (experts - 1) * CAP)
    wait_rows(os, send_sem.at[2], (experts - 1) * CAP)
    wait_rows(ds, send_sem.at[3], experts * CAP)
    for store in stores:
        store.wait()


def solution(mesh):
    tok_spec = P("stage", "expert", None)
    w_spec = P("stage", "expert", None, None)

    def device_step(x_act, route_idx, route_gate, w_up, w_lin, w_down, dy_out):
        _, tokens, width = x_act.shape
        ff = w_up.shape[3]
        slots = 64 * CAP
        groups = 64 // GRP
        any_spec = pl.BlockSpec(memory_space=pl.ANY)
        rows_buf = pltpu.VMEM((slots, width), BF16)
        ff_buf = pltpu.VMEM((slots, ff), BF16)
        dma = pltpu.SemaphoreType.DMA
        outs = pl.pallas_call(
            moe_kernel,
            name="moe",
            out_shape=(
                jax.ShapeDtypeStruct((tokens, width), BF16),
                jax.ShapeDtypeStruct((tokens, width), BF16),
                jax.ShapeDtypeStruct((width, ff), BF16),
                jax.ShapeDtypeStruct((width, ff), BF16),
                jax.ShapeDtypeStruct((ff, width), BF16),
            ),
            in_specs=[any_spec] * 7,
            out_specs=(any_spec,) * 5,
            scratch_shapes=[
                pltpu.VMEM((2, tokens), jnp.int32),
                pltpu.VMEM((2, tokens), F32),
                pltpu.VMEM((tokens, width), BF16),
                pltpu.VMEM((tokens, width), BF16),
                pltpu.VMEM((width, ff), BF16),
                pltpu.VMEM((width, ff), BF16),
                pltpu.VMEM((ff, width), BF16),
                *([rows_buf] * 8),
                *([ff_buf] * 3),
                pltpu.VMEM((8, tokens), F32),
                pltpu.VMEM((8, tokens), F32),
                pltpu.VMEM((2, tokens, 128), F32),
                pltpu.VMEM((4, tokens, 128), F32),
                *([pltpu.VMEM((tokens, width), F32)] * 3),
                pltpu.VMEM((width, ff), BF16),
                pltpu.VMEM((width, ff), BF16),
                pltpu.VMEM((ff, width), BF16),
                pltpu.VMEM((tokens, width), BF16),
                pltpu.VMEM((tokens, width), BF16),
                dma((7,)),
                dma((5,)),
                dma((4,)),
                dma((groups,)),
                dma((groups,)),
                dma((groups,)),
                dma((groups,)),
                dma((2,)),
            ],
            compiler_params=pltpu.CompilerParams(
                collective_id=0, has_side_effects=True, vmem_limit_bytes=66_000_000
            ),
        )(
            jnp.transpose(route_idx[0]), jnp.transpose(route_gate[0]), x_act[0], dy_out[0],
            w_up[0, 0], w_lin[0, 0], w_down[0, 0],
        )
        y_tok, dx_tok, g_up, g_lin, g_down = outs
        return y_tok[None], dx_tok[None], g_up[None, None], g_lin[None, None], g_down[None, None]

    return jax.shard_map(
        device_step,
        mesh=mesh,
        in_specs=(tok_spec, tok_spec, tok_spec, w_spec, w_spec, w_spec, tok_spec),
        out_specs=(tok_spec, tok_spec, w_spec, w_spec, w_spec),
        check_vma=False,
    )
```

profile of v0, /device:TPU:15, one launch (start us, length us, event | category | flops | bytes accessed | tf_op | source)
XLA Modules:
  0.0 88.3 jit_solution(9851212544432692340)
XLA Ops:
  0.6 80.0 %moe.1 = (bf16[512,256]{1,0:T(8,128)(2,1)}, bf16[512,256]{1,0:T(8,128)(2,1)}, bf16[256,2048]{1,0:T(8,128)(2,1)}, bf16[256,2048]{1,0:T(8,128)(2,1)}, bf16[2048,256]{1,0:T(8,128)(2,1)}) custom-call(s32[2,512]{1,0:T(2,128)} %bitcast.26, f32[2,512]{1,0:T(2,128)} %bitcast.27, bf16[512,256]{1,0:T(8,128)(2,1)} %bitcast.22, bf16[512,256]{1,0:T(8,128)(2,1)} %bitcast.23, ...), custom_call_target="tpu_custom_call" | custom-call | tf_op jit(solution)/shard_map/moe/pallas_call | solution.py:310
  80.6 0.0 copy-start.2
  80.7 1.8 %copy.17 = bf16[1,512,256]{2,1,0:T(8,128)(2,1)} copy(bf16[1,512,256]{2,1,0:T(8,128)(2,1)} %bitcast.25) | data formatting | bytes 524288
  82.4 1.7 %copy.18 = bf16[1,512,256]{2,1,0:T(8,128)(2,1)} copy(bf16[1,512,256]{2,1,0:T(8,128)(2,1)} %bitcast.24) | data formatting | bytes 524288
  84.1 0.0 copy-done.2
  84.1 0.0 copy-start.1
  84.1 1.0 %copy.19 = bf16[1,1,256,2048]{3,2,1,0:T(8,128)(2,1)} copy(bf16[1,1,256,2048]{3,2,1,0:T(8,128)(2,1)S(1)} %bitcast.21) | data formatting | bytes 2097152
  85.1 0.6 copy-done.1
  85.7 0.0 copy-start
  85.7 1.0 %copy.20 = bf16[1,1,256,2048]{3,2,1,0:T(8,128)(2,1)} copy(bf16[1,1,256,2048]{3,2,1,0:T(8,128)(2,1)S(1)} %bitcast.20) | data formatting | bytes 2097152
  86.7 0.6 copy-done
  87.3 1.0 %copy.21 = bf16[1,1,2048,256]{3,2,1,0:T(8,128)(2,1)} copy(bf16[1,1,2048,256]{3,2,1,0:T(8,128)(2,1)S(1)} %bitcast.19) | data formatting | bytes 2097152
Async XLA Ops:
  80.6 3.4 %copy-start.2 = (bf16[256,2048]{1,0:T(8,128)(2,1)S(1)}, bf16[256,2048]{1,0:T(8,128)(2,1)}, u32[]{:S(2)}) copy-start(bf16[256,2048]{1,0:T(8,128)(2,1)} %get-tuple-element.12) | copy-start | bytes 3145732
  84.1 1.6 %copy-start.1 = (bf16[256,2048]{1,0:T(8,128)(2,1)S(1)}, bf16[256,2048]{1,0:T(8,128)(2,1)}, u32[]{:S(2)}) copy-start(bf16[256,2048]{1,0:T(8,128)(2,1)} %get-tuple-element.13) | copy-start | bytes 3145732
  85.7 1.6 %copy-start = (bf16[2048,256]{1,0:T(8,128)(2,1)S(1)}, bf16[2048,256]{1,0:T(8,128)(2,1)}, u32[]{:S(2)}) copy-start(bf16[2048,256]{1,0:T(8,128)(2,1)} %get-tuple-element.14) | copy-start | bytes 3145732
where the time goes:
time: 88.5 us; the launch traced here: 88.3 us
  Pallas kernels  80 us (90%)
  local copies, waits for them, and re-layouts  7.6 us (9%)
    pallas_call x1, Pallas kernels, device_step(): pl.pallas_call(moe_kernel, name='moe', out_shape=(jax.ShapeDtypeStruct((t...  80 us
    unnamed x11, local copies, waits for them, and re-layouts  7.6 us

commit v1 on v0

v1 whole, which is shorter than its diff:
```python
import functools

import jax
import jax.numpy as jnp
from jax import lax
from jax.experimental import pallas as pl
from jax.experimental.pallas import tpu as pltpu
from jax.sharding import PartitionSpec as P

MESH = pl.DeviceIdType.MESH
F32 = jnp.float32
BF16 = jnp.bfloat16
CAP = 32
GRP = 8
ROWS = GRP * CAP
FT = 256
RB = 32
NT = (((1,), (1,)), ((), ()))
TN = (((0,), (0,)), ((), ()))


def group_peers(me, group, sign):
    z, y, x = lax.div(me, 16), lax.rem(lax.div(me, 4), 4), lax.rem(me, 4)
    a = lax.div(group, 2)
    b = 2 * (group - 2 * a)
    along_x = [lax.rem(x + 8 + sign * k, 4) for k in range(4)]
    along_y = [4 * lax.rem(y + 8 + sign * (a + k), 4) for k in range(4)]
    along_z = [16 * lax.rem(z + 8 + sign * (b + k), 4) for k in range(4)]
    return [along_x[n % 4] + along_y[n % 4] + along_z[(n % 4 + n // 4) % 4] for n in range(GRP)]


def slot_ids(me, group, shape, dim):
    n = lax.broadcasted_iota(jnp.int32, shape, dim)
    q = n // CAP + group * GRP
    a, b, c = q >> 4, (q >> 2) & 3, q & 3
    z = (me // 16 + c + b) & 3
    y = (me // 4 + c + a) & 3
    x = (me + c) & 3
    return ((z * 16 + y * 4 + x) * CAP + (n & (CAP - 1))).astype(F32)


def moe_kernel(
    idx_hbm, gate_hbm, x_hbm, dy_hbm, wup_hbm, wlin_hbm, wdn_hbm,
    sum0, sum1, sumx, par, gup, glin, gdn,
    idx_v, gate_v, x_v, dy_v, wup, wlin, wdn,
    xs, xr, us, ur, os, orr, ds, dr,
    hid, dup, dlin, x_t, u_t, own, pick_x, pick_0, pick_1,
    in_sem, send_sem, x_sem, u_sem, o_sem, d_sem, pack_sem,
):
    me = lax.axis_index("expert")
    stage = lax.axis_index("stage")
    other = 1 - stage
    tokens = x_v.shape[0]
    experts = 64
    groups = experts // GRP
    ff = wup.shape[1]

    loads = [
        pltpu.make_async_copy(src, dst, in_sem.at[n])
        for n, (src, dst) in enumerate(
            ((idx_hbm, idx_v), (x_hbm, x_v), (gate_hbm, gate_v), (dy_hbm, dy_v), (wup_hbm, wup), (wlin_hbm, wlin), (wdn_hbm, wdn))
        )
    ]
    for load in loads:
        load.start()

    barrier = pltpu.get_barrier_semaphore()

    pl.semaphore_signal(barrier, inc=1, device_id=(other, me), device_id_type=MESH)

    def greet(n, carry):
        for k in range(7):
            peer = me + (n * 7 + k + 1)
            peer = peer - jnp.where(peer >= experts, experts, 0)
            for side in (stage, other):
                pl.semaphore_signal(barrier, inc=1, device_id=(side, peer), device_id_type=MESH)
        return carry

    lax.fori_loop(0, experts // 7, greet, 0)

    def send_group(src, dst, kind, sem, group, dest_stage, sign, skip_self):
        peers = group_peers(me, jnp.int32(group), sign)
        for place in range(GRP):
            if place == 0 and skip_self and isinstance(group, int) and group == 0:
                continue
            rows = pl.ds(pl.multiple_of((group * GRP + place) * CAP, CAP), CAP)
            pltpu.make_async_remote_copy(
                src_ref=src.at[rows],
                dst_ref=dst.at[rows],
                send_sem=send_sem.at[kind],
                recv_sem=sem.at[group],
                device_id=(dest_stage, peers[place]),
                device_id_type=MESH,
            ).start()

    def wait_rows(buf, sem, rows):
        pltpu.make_async_copy(buf.at[pl.ds(0, rows)], buf.at[pl.ds(0, rows)], sem).wait()

    def wait_group(buf, sem, group, skip_self):
        own_slot = skip_self and isinstance(group, int) and group == 0
        wait_rows(buf, sem.at[group], ROWS - CAP if own_slot else ROWS)

    send_x = functools.partial(send_group, xs, xr, 0, x_sem, dest_stage=other, sign=1, skip_self=False)
    send_u = functools.partial(send_group, us, ur, 1, u_sem, dest_stage=stage, sign=1, skip_self=True)
    send_o = functools.partial(send_group, os, orr, 2, o_sem, dest_stage=stage, sign=-1, skip_self=True)
    send_d = functools.partial(send_group, ds, dr, 3, d_sem, dest_stage=other, sign=-1, skip_self=False)

    loads[0].wait()
    expert_row = lax.broadcasted_iota(jnp.int32, (experts, tokens), 0)
    chosen = [(idx_v[pl.ds(j, 1), :] == expert_row).astype(F32) for j in range(2)]
    before = lax.broadcasted_iota(jnp.int32, (tokens, tokens), 0) < lax.broadcasted_iota(jnp.int32, (tokens, tokens), 1)
    earlier = jnp.dot(
        (chosen[0] + chosen[1]).astype(BF16), jnp.where(before, 1.0, 0.0).astype(BF16), preferred_element_type=F32
    )
    place = earlier + CAP * expert_row.astype(F32)
    loads[2].wait()
    for j in range(2):
        own[pl.ds(j, 1), :] = jnp.sum(chosen[j] * place, axis=0, keepdims=True)
        own[pl.ds(2 + j, 1), :] = gate_v[pl.ds(j, 1), :]
    own[pl.ds(4, 4), :] = jnp.zeros((4, tokens), F32)

    def slot_mask(route, group):
        slots = slot_ids(me, group, (ROWS, 128), 0)
        slots = jnp.concatenate([slots] * (tokens // 128), axis=1)
        return [slots == route[pl.ds(j, 1), :] for j in range(2)]

    def rows_of(group):
        return pl.ds(pl.multiple_of(group * ROWS, ROWS), ROWS)

    def x_block(group):
        rows = rows_of(group)
        hit = slot_mask(own, group)
        pick = jnp.where(hit[0] | hit[1], 1.0, 0.0).astype(BF16)
        pick_x[rows, :] = pick
        xs[rows, :] = jnp.dot(pick, x_v[...], preferred_element_type=F32).astype(BF16)

    def u_block(group):
        rows = rows_of(group)
        hit = slot_mask(par, group)
        picks = [jnp.where(h, 1.0, 0.0) for h in hit]
        gates = picks[0] * par[pl.ds(2, 1), :] + picks[1] * par[pl.ds(3, 1), :]
        gates = jnp.sum(gates, axis=1, keepdims=True)
        pick_0[rows, :] = picks[0].astype(BF16)
        pick_1[rows, :] = picks[1].astype(BF16)
        pick = (picks[0] + picks[1]).astype(BF16)
        us[rows, :] = (gates * jnp.dot(pick, dy_v[...], preferred_element_type=F32)).astype(BF16)

    loads[1].wait()
    x_block(0)
    x_block(1)
    pl.semaphore_wait(barrier, 2 * experts - 1)
    pack = pltpu.make_async_remote_copy(
        src_ref=own, dst_ref=par, send_sem=pack_sem.at[0], recv_sem=pack_sem.at[1],
        device_id=(other, me), device_id_type=MESH,
    )
    pack.start()
    send_x(0)
    x_block(2)
    send_x(1)
    loads[3].wait()
    pack.wait()
    u_block(0)
    ur[pl.ds(0, CAP), :] = us[pl.ds(0, CAP), :]
    x_block(3)
    send_x(2)
    send_u(0)

    def feed(group, carry):
        u_block(group)
        x_block(group + 3)
        send_x(group + 2)

        @pl.when(group > 1)
        def _():
            send_u(group - 1)

        return carry

    lax.fori_loop(1, groups - 3, feed, 0)

    def feed_u(group, carry):
        send_u(group - 1)
        u_block(group)
        return carry

    send_x(groups - 1)
    lax.fori_loop(groups - 3, groups, feed_u, 0)
    for n in range(4, 7):
        loads[n].wait()
    send_u(groups - 1)

    def work(group):
        rows = rows_of(group)
        wait_group(xr, x_sem, group, False)
        wait_group(ur, u_sem, group, True)
        x_in, u_in = xr[rows, :], ur[rows, :]
        x_t[:, rows] = jnp.transpose(x_in, (1, 0))
        u_t[:, rows] = jnp.transpose(u_in, (1, 0))
        for n in range(ff // FT):
            cols = pl.ds(n * FT, FT)
            all_up = jnp.dot(x_in, wup[:, cols], preferred_element_type=F32)
            all_lin = jnp.dot(x_in, wlin[:, cols], preferred_element_type=F32)
            all_d = lax.dot_general(u_in, wdn[cols, :], NT, preferred_element_type=F32)
            for r in range(0, ROWS, RB):
                part = pl.ds(pl.multiple_of(group * ROWS + r, RB), RB)
                pre_up, pre_lin = all_up[r : r + RB], all_lin[r : r + RB]
                d_hid = all_d[r : r + RB].astype(BF16).astype(F32)
                sig = jax.nn.sigmoid(pre_up)
                act = pre_up * sig
                hid[part, cols] = (act * pre_lin).astype(BF16)
                dup[part, cols] = (d_hid * pre_lin * sig * (1.0 + pre_up * (1.0 - sig))).astype(BF16)
                dlin[part, cols] = (d_hid * act).astype(BF16)
        os[rows, :] = jnp.dot(hid[rows, :], wdn[...], preferred_element_type=F32).astype(BF16)
        d_in = lax.dot_general(dup[rows, :], wup[...], NT, preferred_element_type=F32)
        d_in += lax.dot_general(dlin[rows, :], wlin[...], NT, preferred_element_type=F32)
        send_o(group)
        ds[rows, :] = d_in.astype(BF16)

    work(0)
    orr[pl.ds(0, CAP), :] = os[pl.ds(0, CAP), :]

    def work_next(group, carry):
        work(group)
        send_d(group - 1)
        return carry

    lax.fori_loop(1, groups, work_next, 0)

    def weight_grads(n, carry):
        cols = pl.ds(pl.multiple_of(n * 256, 256), 256)
        gup[:, cols] = jnp.dot(x_t[...], dup[:, cols], preferred_element_type=F32).astype(BF16)
        glin[:, cols] = jnp.dot(x_t[...], dlin[:, cols], preferred_element_type=F32).astype(BF16)
        gdn[cols, :] = jnp.transpose(jnp.dot(u_t[...], hid[:, cols], preferred_element_type=F32), (1, 0)).astype(BF16)
        return carry

    weight_grads(0, 0)
    send_d(groups - 1)
    lax.fori_loop(1, ff // 256, weight_grads, 0)

    def merge(group, first):
        rows = rows_of(group)

        def add(total, rows_in, pick):
            part = lax.dot_general(rows_in, pick, TN, preferred_element_type=F32)
            total[...] = part if first else total[...] + part

        wait_group(orr, o_sem, group, True)
        rows_o = orr[rows, :]
        add(sum0, rows_o, pick_0[rows, :])
        add(sum1, rows_o, pick_1[rows, :])
        wait_group(dr, d_sem, group, False)
        add(sumx, dr[rows, :], pick_x[rows, :])

    merge(0, True)

    def merge_next(group, carry):
        merge(group, False)
        return carry

    lax.fori_loop(1, groups, merge_next, 0)
    wait_rows(xs, send_sem.at[0], experts * CAP)
    wait_rows(us, send_sem.at[1], (experts - 1) * CAP)
    wait_rows(os, send_sem.at[2], (experts - 1) * CAP)
    wait_rows(ds, send_sem.at[3], experts * CAP)


def finish_kernel(
    sum0, sum1, sumx, route, gup, glin, gdn,
    y_hbm, dx_hbm, gup_hbm, glin_hbm, gdn_hbm, y_v, dx_v, sem,
):
    pairs = ((gup, gup_hbm), (glin, glin_hbm), (gdn, gdn_hbm), (y_v, y_hbm), (dx_v, dx_hbm))
    stores = [pltpu.make_async_copy(src, dst, sem.at[n]) for n, (src, dst) in enumerate(pairs)]
    for n in range(3):
        stores[n].start()
    y_t = route[pl.ds(2, 1), :] * sum0[...] + route[pl.ds(3, 1), :] * sum1[...]
    y_v[...] = jnp.transpose(y_t, (1, 0)).astype(BF16)
    stores[3].start()
    dx_v[...] = jnp.transpose(sumx[...], (1, 0)).astype(BF16)
    stores[4].start()
    for store in stores:
        store.wait()


def solution(mesh):
    tok_spec = P("stage", "expert", None)
    w_spec = P("stage", "expert", None, None)

    def device_step(x_act, route_idx, route_gate, w_up, w_lin, w_down, dy_out):
        _, tokens, width = x_act.shape
        ff = w_up.shape[3]
        slots = 64 * CAP
        groups = 64 // GRP
        any_spec = pl.BlockSpec(memory_space=pl.ANY)
        rows_buf = pltpu.VMEM((slots, width), BF16)
        ff_buf = pltpu.VMEM((slots, ff), BF16)
        dma = pltpu.SemaphoreType.DMA
        any_specs = [any_spec] * 5
        vmem_spec = pl.BlockSpec(memory_space=pltpu.VMEM)
        held = pl.pallas_call(
            moe_kernel,
            name="moe",
            out_shape=(
                *([pltpu.VMEM((width, tokens), F32)] * 3),
                pltpu.VMEM((8, tokens), F32),
                pltpu.VMEM((width, ff), BF16),
                pltpu.VMEM((width, ff), BF16),
                pltpu.VMEM((ff, width), BF16),
            ),
            in_specs=[any_spec] * 7,
            out_specs=(vmem_spec,) * 7,
            scratch_shapes=[
                pltpu.VMEM((2, tokens), jnp.int32),
                pltpu.VMEM((2, tokens), F32),
                pltpu.VMEM((tokens, width), BF16),
                pltpu.VMEM((tokens, width), BF16),
                pltpu.VMEM((width, ff), BF16),
                pltpu.VMEM((width, ff), BF16),
                pltpu.VMEM((ff, width), BF16),
                *([rows_buf] * 8),
                *([ff_buf] * 3),
                *([pltpu.VMEM((width, slots), BF16)] * 2),
                pltpu.VMEM((8, tokens), F32),
                *([pltpu.VMEM((slots, tokens), BF16)] * 3),
                dma((7,)),
                dma((4,)),
                dma((groups,)),
                dma((groups,)),
                dma((groups,)),
                dma((groups,)),
                dma((2,)),
            ],
            compiler_params=pltpu.CompilerParams(
                collective_id=0, has_side_effects=True, vmem_limit_bytes=56 * 2**20
            ),
        )(
            jnp.transpose(route_idx[0]), jnp.transpose(route_gate[0]), x_act[0], dy_out[0],
            w_up[0, 0], w_lin[0, 0], w_down[0, 0],
        )
        outs = pl.pallas_call(
            finish_kernel,
            name="finish",
            out_shape=(
                jax.ShapeDtypeStruct((tokens, width), BF16),
                jax.ShapeDtypeStruct((tokens, width), BF16),
                jax.ShapeDtypeStruct((width, ff), BF16),
                jax.ShapeDtypeStruct((width, ff), BF16),
                jax.ShapeDtypeStruct((ff, width), BF16),
            ),
            in_specs=[vmem_spec] * 7,
            out_specs=any_specs,
            scratch_shapes=[pltpu.VMEM((tokens, width), BF16), pltpu.VMEM((tokens, width), BF16), dma((5,))],
            compiler_params=pltpu.CompilerParams(vmem_limit_bytes=4 * 2**20),
        )(*held)
        y_tok, dx_tok, g_up, g_lin, g_down = outs
        return y_tok[None], dx_tok[None], g_up[None, None], g_lin[None, None], g_down[None, None]

    return jax.shard_map(
        device_step,
        mesh=mesh,
        in_specs=(tok_spec, tok_spec, tok_spec, w_spec, w_spec, w_spec, tok_spec),
        out_specs=(tok_spec, tok_spec, w_spec, w_spec, w_spec),
        check_vma=False,
    )
```

time: 88.5 us -> 76.5 us (0.86)
  the two profiles are of different devices: /device:TPU:15 before, /device:TPU:8 now
where the time goes in v1:
time: 76.5 us; the launch traced here: 76.4 us
  Pallas kernels  75.8 us (99%)
    pallas_call x1, Pallas kernels, device_step(): pl.pallas_call(moe_kernel, name='moe', out_shape=(*[pltpu.VMEM((width, to...  73.9 us
    pallas_call x1, Pallas kernels, device_step(): pl.pallas_call(finish_kernel, name='finish', out_shape=(jax.ShapeDtypeStr...  1.87 us

profile of v1, /device:TPU:8, one launch (start us, length us, event | category | flops | bytes accessed | tf_op | source)
XLA Modules:
  0.0 76.4 jit_solution(9913568866938577498)
XLA Ops:
  0.6 73.9 %moe.1 = (f32[256,512]{1,0:T(8,128)S(1)}, f32[256,512]{1,0:T(8,128)S(1)}, f32[256,512]{1,0:T(8,128)S(1)}, f32[8,512]{1,0:T(8,128)S(1)}, bf16[256,2048]{1,0:T(8,1...) custom-call(s32[2,512]{1,0:T(2,128)} %bitcast.21, f32[2,512]{1,0:T(2,128)} %bitcast.22, ...), custom_call_target="tpu_custom_call" | custom-call | tf_op jit(solution)/shard_map/moe/pallas_call | solution.py:299
  74.5 1.9 %finish.1 = (bf16[512,256]{1,0:T(8,128)(2,1)}, bf16[512,256]{1,0:T(8,128)(2,1)}, bf16[256,2048]{1,0:T(8,128)(2,1)}, bf16[256,2048]{1,0:T(8,128)(2,1)}, bf16[2048,256]{1,0:T(8,128)(2,1)}) custom-call(f32[256,512]{1,0:T(8,128)S(1)} %get-tuple-element.17.sum0, f32[256,512]{1,0:T(8,128)S(1)} %get-tuple-element.18.sum1, f32[256,512]{1,0:T(8,128)S(1)} %get-tuple-element.19.sumx, ...), custom_call_target="tpu_custom_call" | custom-call | tf_op jit(solution)/shard_map/finish/pallas_call | solution.py:339

commit v2 on v1

--- a/solution.py
+++ b/solution.py
@@ -15,6 +15,8 @@
 ROWS = GRP * CAP
 FT = 256
 RB = 32
+HOLD = 5
+AHEAD = 4
 NT = (((1,), (1,)), ((), ()))
 TN = (((0,), (0,)), ((), ()))
 
@@ -66,17 +68,15 @@
 
     barrier = pltpu.get_barrier_semaphore()
 
-    pl.semaphore_signal(barrier, inc=1, device_id=(other, me), device_id_type=MESH)
-
-    def greet(n, carry):
-        for k in range(7):
-            peer = me + (n * 7 + k + 1)
-            peer = peer - jnp.where(peer >= experts, experts, 0)
-            for side in (stage, other):
+    z, y, x = lax.div(me, 16), lax.rem(lax.div(me, 4), 4), lax.rem(me, 4)
+    ring = [[lax.rem(pos + k, 4) * unit for k in range(4)] for pos, unit in ((z, 16), (y, 4), (x, 1))]
+    hops = (0, 1, 2, 1)
+    steps = [(i, j, k) for i in range(4) for j in range(4) for k in range(4)]
+    for i, j, k in sorted(steps, key=lambda n: -sum(hops[m] for m in n)):
+        peer = ring[0][i] + ring[1][j] + ring[2][k]
+        for side in (stage, other):
+            if (i, j, k) != (0, 0, 0) or side is other:
                 pl.semaphore_signal(barrier, inc=1, device_id=(side, peer), device_id_type=MESH)
-        return carry
-
-    lax.fori_loop(0, experts // 7, greet, 0)
 
     def send_group(src, dst, kind, sem, group, dest_stage, sign, skip_self):
         peers = group_peers(me, jnp.int32(group), sign)
@@ -159,40 +159,44 @@
     send_x(1)
     loads[3].wait()
     pack.wait()
-    u_block(0)
-    ur[pl.ds(0, CAP), :] = us[pl.ds(0, CAP), :]
-    x_block(3)
-    send_x(2)
-    send_u(0)
+    for group in range(AHEAD):
+        u_block(group)
+        if group == 0:
+            ur[pl.ds(0, CAP), :] = us[pl.ds(0, CAP), :]
+        if group + 3 < groups:
+            x_block(group + 3)
+        if group + 2 < AHEAD:
+            send_x(group + 2)
+        send_u(group)
 
     def feed(group, carry):
         u_block(group)
-        x_block(group + 3)
-        send_x(group + 2)
-
-        @pl.when(group > 1)
+
+        @pl.when(group + 3 < groups)
         def _():
-            send_u(group - 1)
-
-        return carry
-
-    lax.fori_loop(1, groups - 3, feed, 0)
-
-    def feed_u(group, carry):
-        send_u(group - 1)
-        u_block(group)
-        return carry
-
-    send_x(groups - 1)
-    lax.fori_loop(groups - 3, groups, feed_u, 0)
+            x_block(group + 3)
+
+        return carry
+
+    lax.fori_loop(AHEAD, groups, feed, 0)
     for n in range(4, 7):
         loads[n].wait()
-    send_u(groups - 1)
-
-    def work(group):
+
+    def work(group, send):
         rows = rows_of(group)
         wait_group(xr, x_sem, group, False)
         wait_group(ur, u_sem, group, True)
+        if isinstance(group, int):
+            if group + AHEAD < groups:
+                send_x(group + AHEAD)
+                send_u(group + AHEAD)
+        elif AHEAD < groups:
+
+            @pl.when(group + AHEAD < groups)
+            def _():
+                send_x(group + AHEAD)
+                send_u(group + AHEAD)
+
         x_in, u_in = xr[rows, :], ur[rows, :]
         x_t[:, rows] = jnp.transpose(x_in, (1, 0))
         u_t[:, rows] = jnp.transpose(u_in, (1, 0))
@@ -213,18 +217,32 @@
         os[rows, :] = jnp.dot(hid[rows, :], wdn[...], preferred_element_type=F32).astype(BF16)
         d_in = lax.dot_general(dup[rows, :], wup[...], NT, preferred_element_type=F32)
         d_in += lax.dot_general(dlin[rows, :], wlin[...], NT, preferred_element_type=F32)
+        if send:
+            send_o(group)
+        ds[rows, :] = d_in.astype(BF16)
+
+    work(0, False)
+    orr[pl.ds(0, CAP), :] = os[pl.ds(0, CAP), :]
+
+    def work_hold(group, carry):
+        work(group, False)
+        return carry
+
+    def release(group, carry):
         send_o(group)
-        ds[rows, :] = d_in.astype(BF16)
-
-    work(0)
-    orr[pl.ds(0, CAP), :] = os[pl.ds(0, CAP), :]
+        send_d(group)
+        return carry
 
     def work_next(group, carry):
-        work(group)
+        work(group, True)
         send_d(group - 1)
         return carry
 
-    lax.fori_loop(1, groups, work_next, 0)
+    lax.fori_loop(1, HOLD, work_hold, 0)
+    release(0, 0)
+    lax.fori_loop(1, HOLD - 1, release, 0)
+    send_o(HOLD - 1)
+    lax.fori_loop(HOLD, groups, work_next, 0)
 
     def weight_grads(n, carry):
         cols = pl.ds(pl.multiple_of(n * 256, 256), 256)
@@ -237,27 +255,23 @@
     send_d(groups - 1)
     lax.fori_loop(1, ff // 256, weight_grads, 0)
 
-    def merge(group, first):
-        rows = rows_of(group)
-
-        def add(total, rows_in, pick):
-            part = lax.dot_general(rows_in, pick, TN, preferred_element_type=F32)
-            total[...] = part if first else total[...] + part
-
-        wait_group(orr, o_sem, group, True)
-        rows_o = orr[rows, :]
-        add(sum0, rows_o, pick_0[rows, :])
-        add(sum1, rows_o, pick_1[rows, :])
-        wait_group(dr, d_sem, group, False)
-        add(sumx, dr[rows, :], pick_x[rows, :])
-
-    merge(0, True)
-
-    def merge_next(group, carry):
-        merge(group, False)
-        return carry
-
-    lax.fori_loop(1, groups, merge_next, 0)
+    def merge(lo, hi):
+        rows = pl.ds(lo * ROWS, (hi - lo) * ROWS)
+
+        def add(total, buf, pick):
+            part = lax.dot_general(buf[rows, :], pick[rows, :], TN, preferred_element_type=F32)
+            total[...] = part if lo == 0 else total[...] + part
+
+        for group in range(lo, hi):
+            wait_group(orr, o_sem, group, True)
+        add(sum0, orr, pick_0)
+        add(sum1, orr, pick_1)
+        for group in range(lo, hi):
+            wait_group(dr, d_sem, group, False)
+        add(sumx, dr, pick_x)
+
+    merge(0, 4)
+    merge(4, groups)
     wait_rows(xs, send_sem.at[0], experts * CAP)
     wait_rows(us, send_sem.at[1], (experts - 1) * CAP)
     wait_rows(os, send_sem.at[2], (experts - 1) * CAP)

time: 76.5 us -> 72.3 us (0.945)
  the two profiles are of different devices: /device:TPU:8 before, /device:TPU:3 now
where the time goes in v2:
time: 72.3 us; the launch traced here: 72.2 us
  Pallas kernels  71.4 us (99%)
  between operations  0.8 us (1%)
    pallas_call x1, Pallas kernels, device_step(): pl.pallas_call(moe_kernel, name='moe', out_shape=(*[pltpu.VMEM((width, to...  69.5 us
    pallas_call x1, Pallas kernels, device_step(): pl.pallas_call(finish_kernel, name='finish', out_shape=(jax.ShapeDtypeStr...  1.87 us

profile of v2, /device:TPU:3, one launch (start us, length us, event | category | flops | bytes accessed | tf_op | source)
XLA Modules:
  0.0 72.2 jit_solution(15740269023997267426)
XLA Ops:
  0.6 69.5 %moe.1 = (f32[256,512]{1,0:T(8,128)S(1)}, f32[256,512]{1,0:T(8,128)S(1)}, f32[256,512]{1,0:T(8,128)S(1)}, f32[8,512]{1,0:T(8,128)S(1)}, bf16[256,2048]{1,0:T(8,1...) custom-call(s32[2,512]{1,0:T(2,128)} %bitcast.21, f32[2,512]{1,0:T(2,128)} %bitcast.22, ...), custom_call_target="tpu_custom_call" | custom-call | tf_op jit(solution)/shard_map/moe/pallas_call | solution.py:313
  70.2 1.9 %finish.1 = (bf16[512,256]{1,0:T(8,128)(2,1)}, bf16[512,256]{1,0:T(8,128)(2,1)}, bf16[256,2048]{1,0:T(8,128)(2,1)}, bf16[256,2048]{1,0:T(8,128)(2,1)}, bf16[2048,256]{1,0:T(8,128)(2,1)}) custom-call(f32[256,512]{1,0:T(8,128)S(1)} %get-tuple-element.17.sum0, f32[256,512]{1,0:T(8,128)S(1)} %get-tuple-element.18.sum1, f32[256,512]{1,0:T(8,128)S(1)} %get-tuple-element.19.sumx, ...), custom_call_target="tpu_custom_call" | custom-call | tf_op jit(solution)/shard_map/finish/pallas_call | solution.py:353

commit v3 on v2

--- a/solution.py
+++ b/solution.py
@@ -16,7 +16,7 @@
 FT = 256
 RB = 32
 HOLD = 5
-AHEAD = 4
+AHEAD = 6
 NT = (((1,), (1,)), ((), ()))
 TN = (((0,), (0,)), ((), ()))
 
@@ -146,8 +146,12 @@
         us[rows, :] = (gates * jnp.dot(pick, dy_v[...], preferred_element_type=F32)).astype(BF16)
 
     loads[1].wait()
-    x_block(0)
-    x_block(1)
+
+    def fill_x(group, carry):
+        x_block(group)
+        return carry
+
+    lax.fori_loop(0, groups, fill_x, 0)
     pl.semaphore_wait(barrier, 2 * experts - 1)
     pack = pltpu.make_async_remote_copy(
         src_ref=own, dst_ref=par, send_sem=pack_sem.at[0], recv_sem=pack_sem.at[1],
@@ -155,7 +159,6 @@
     )
     pack.start()
     send_x(0)
-    x_block(2)
     send_x(1)
     loads[3].wait()
     pack.wait()
@@ -163,22 +166,18 @@
         u_block(group)
         if group == 0:
             ur[pl.ds(0, CAP), :] = us[pl.ds(0, CAP), :]
-        if group + 3 < groups:
-            x_block(group + 3)
-        if group + 2 < AHEAD:
-            send_x(group + 2)
-        send_u(group)
-
-    def feed(group, carry):
+        if group > 0:
+            send_u(group - 1)
+        if 1 < group:
+            send_x(group)
+
+    def fill_u(group, carry):
         u_block(group)
-
-        @pl.when(group + 3 < groups)
-        def _():
-            x_block(group + 3)
-
-        return carry
-
-    lax.fori_loop(AHEAD, groups, feed, 0)
+        return carry
+
+    u_block(AHEAD)
+    send_u(AHEAD - 1)
+    lax.fori_loop(AHEAD + 1, groups, fill_u, 0)
     for n in range(4, 7):
         loads[n].wait()
 
@@ -228,21 +227,21 @@
         work(group, False)
         return carry
 
-    def release(group, carry):
+    def release(group):
         send_o(group)
         send_d(group)
-        return carry
 
     def work_next(group, carry):
-        work(group, True)
-        send_d(group - 1)
-        return carry
-
-    lax.fori_loop(1, HOLD, work_hold, 0)
-    release(0, 0)
-    lax.fori_loop(1, HOLD - 1, release, 0)
-    send_o(HOLD - 1)
-    lax.fori_loop(HOLD, groups, work_next, 0)
+        work(group, False)
+        release(2 * group - 8)
+        release(2 * group - 7)
+        return carry
+
+    lax.fori_loop(1, 4, work_hold, 0)
+    work(4, False)
+    for group in range(2):
+        release(group)
+    lax.fori_loop(4+1, groups, work_next, 0)
 
     def weight_grads(n, carry):
         cols = pl.ds(pl.multiple_of(n * 256, 256), 256)
@@ -251,9 +250,7 @@
         gdn[cols, :] = jnp.transpose(jnp.dot(u_t[...], hid[:, cols], preferred_element_type=F32), (1, 0)).astype(BF16)
         return carry
 
-    weight_grads(0, 0)
-    send_d(groups - 1)
-    lax.fori_loop(1, ff // 256, weight_grads, 0)
+    lax.fori_loop(0, ff // 256, weight_grads, 0)
 
     def merge(lo, hi):
         rows = pl.ds(lo * ROWS, (hi - lo) * ROWS)

time: 72.3 us -> 70.2 us (0.971)
  the two profiles are of different devices: /device:TPU:3 before, /device:TPU:1 now
where the time goes in v3:
time: 70.2 us; the launch traced here: 70 us
  Pallas kernels  69.2 us (99%)
  between operations  0.8 us (1%)
    pallas_call x1, Pallas kernels, device_step(): pl.pallas_call(moe_kernel, name='moe', out_shape=(*[pltpu.VMEM((width, to...  67.4 us
    pallas_call x1, Pallas kernels, device_step(): pl.pallas_call(finish_kernel, name='finish', out_shape=(jax.ShapeDtypeStr...  1.87 us

profile of v3, /device:TPU:1, one launch (start us, length us, event | category | flops | bytes accessed | tf_op | source)
XLA Modules:
  0.0 70.0 jit_solution(12275457817400170917)
XLA Ops:
  0.6 67.4 %moe.1 = (f32[256,512]{1,0:T(8,128)S(1)}, f32[256,512]{1,0:T(8,128)S(1)}, f32[256,512]{1,0:T(8,128)S(1)}, f32[8,512]{1,0:T(8,128)S(1)}, bf16[256,2048]{1,0:T(8,1...) custom-call(s32[2,512]{1,0:T(2,128)} %bitcast.21, f32[2,512]{1,0:T(2,128)} %bitcast.22, ...), custom_call_target="tpu_custom_call" | custom-call | tf_op jit(solution)/shard_map/moe/pallas_call | solution.py:310
  68.0 1.9 %finish.1 = (bf16[512,256]{1,0:T(8,128)(2,1)}, bf16[512,256]{1,0:T(8,128)(2,1)}, bf16[256,2048]{1,0:T(8,128)(2,1)}, bf16[256,2048]{1,0:T(8,128)(2,1)}, bf16[2048,256]{1,0:T(8,128)(2,1)}) custom-call(f32[256,512]{1,0:T(8,128)S(1)} %get-tuple-element.17.sum0, f32[256,512]{1,0:T(8,128)S(1)} %get-tuple-element.18.sum1, f32[256,512]{1,0:T(8,128)S(1)} %get-tuple-element.19.sumx, ...), custom_call_target="tpu_custom_call" | custom-call | tf_op jit(solution)/shard_map/finish/pallas_call | solution.py:350

commit v4 on v3

--- a/solution.py
+++ b/solution.py
@@ -267,8 +267,8 @@
             wait_group(dr, d_sem, group, False)
         add(sumx, dr, pick_x)
 
-    merge(0, 4)
-    merge(4, groups)
+    merge(0, 6)
+    merge(6, groups)
     wait_rows(xs, send_sem.at[0], experts * CAP)
     wait_rows(us, send_sem.at[1], (experts - 1) * CAP)
     wait_rows(os, send_sem.at[2], (experts - 1) * CAP)

time: 70.2 us -> 70 us (level)
  no operation moved by 1% of the time
where the time goes in v4:
time: 70 us; the launch traced here: 69.9 us
  Pallas kernels  69.1 us (99%)
  between operations  0.8 us (1%)
    pallas_call x1, Pallas kernels, device_step(): pl.pallas_call(moe_kernel, name='moe', out_shape=(*[pltpu.VMEM((width, to...  67.2 us
    pallas_call x1, Pallas kernels, device_step(): pl.pallas_call(finish_kernel, name='finish', out_shape=(jax.ShapeDtypeStr...  1.87 us

profile of v4, /device:TPU:1, one launch (start us, length us, event | category | flops | bytes accessed | tf_op | source)
XLA Modules:
  0.0 69.9 jit_solution(910488782374787570)
XLA Ops:
  0.6 67.2 %moe.1 = (f32[256,512]{1,0:T(8,128)S(1)}, f32[256,512]{1,0:T(8,128)S(1)}, f32[256,512]{1,0:T(8,128)S(1)}, f32[8,512]{1,0:T(8,128)S(1)}, bf16[256,2048]{1,0:T(8,1...) custom-call(s32[2,512]{1,0:T(2,128)} %bitcast.21, f32[2,512]{1,0:T(2,128)} %bitcast.22, ...), custom_call_target="tpu_custom_call" | custom-call | tf_op jit(solution)/shard_map/moe/pallas_call | solution.py:310
  67.9 1.9 %finish.1 = (bf16[512,256]{1,0:T(8,128)(2,1)}, bf16[512,256]{1,0:T(8,128)(2,1)}, bf16[256,2048]{1,0:T(8,128)(2,1)}, bf16[256,2048]{1,0:T(8,128)(2,1)}, bf16[2048,256]{1,0:T(8,128)(2,1)}) custom-call(f32[256,512]{1,0:T(8,128)S(1)} %get-tuple-element.17.sum0, f32[256,512]{1,0:T(8,128)S(1)} %get-tuple-element.18.sum1, f32[256,512]{1,0:T(8,128)S(1)} %get-tuple-element.19.sumx, ...), custom_call_target="tpu_custom_call" | custom-call | tf_op jit(solution)/shard_map/finish/pallas_call | solution.py:350
